TPU v7x, 256 devices: a whole 4x4x8 slice. The times are simulated.
256 devices in a mesh: dp: 16 (over z_hi, x, core), space: 16 (over y, z_lo).
Axes of the slice: x: 4, y: 4, z: 8 (z_hi: 2, z_lo: 4; z = z_hi * 4 + z_lo), core: 2. Of those that a mesh axis runs over, the one named last changes fastest.
Arguments:
- section_three: bfloat16 [16, 128, 128, 512], P('dp', 'space'), parts along dimension 0, may hold values from -6 to 6
- section_four: bfloat16 [16, 64, 64, 1024], P('dp', 'space'), parts along dimension 0, may hold values from -6 to 6
- section_five: bfloat16 [16, 32, 32, 2048], P('dp', 'space'), parts along dimension 0, may hold values from -6 to 6
- lateral_three: bfloat16 [512, 256], P('space'), may hold values from -0.25 to 0.25
- lateral_four: bfloat16 [1024, 256], P('space'), may hold values from -0.1875 to 0.1875
- lateral_five: bfloat16 [2048, 256], P('space'), may hold values from -0.125 to 0.125
- lateral_bias_three: float32 [256], replicated, may hold values from -3 to 3
- lateral_bias_four: float32 [256], replicated, may hold values from -3 to 3
- lateral_bias_five: float32 [256], replicated, may hold values from -3 to 3
- output_three: bfloat16 [3, 3, 256, 256], P(None, None, 'space'), may hold values from -0.125 to 0.125
- output_four: bfloat16 [3, 3, 256, 256], P(None, None, 'space'), may hold values from -0.125 to 0.125
- output_five: bfloat16 [3, 3, 256, 256], P(None, None, 'space'), may hold values from -0.125 to 0.125
- output_bias_three: float32 [256], replicated, may hold values from -3 to 3
- output_bias_four: float32 [256], replicated, may hold values from -3 to 3
- output_bias_five: float32 [256], replicated, may hold values from -3 to 3
Outputs:
- level_three: bfloat16 [16, 128, 128, 256], P('dp', 'space'), parts along dimension 0
- level_four: bfloat16 [16, 64, 64, 256], P('dp', 'space'), parts along dimension 0
- level_five: bfloat16 [16, 32, 32, 256], P('dp'), parts along dimension 0
- level_six: bfloat16 [16, 16, 16, 256], P('dp'), parts along dimension 0
There are 16 independent parts, one for each index of `dp`. A program takes and returns all parts, laid end to end along the dimension named above; an argument that names none is the same for every part. Nothing has to cross between parts.
All inputs are finite; a program needn't handle non-finite values.
Results may differ from a plain program's by a relative error of at most 0.0095.
Values may be sent and summed in bfloat16 or wider, within the bound.
A program may use at most 64 MiB of HBM per device.

v0:
```python
import jax
import jax.numpy as jnp
from jax import lax
from jax.sharding import PartitionSpec as P


def shifted(array, axis, by):
    count = lax.axis_size(axis)
    pairs = [(i, i + by) for i in range(count) if 0 <= i + by < count]
    return lax.ppermute(array, axis, pairs)


def joined_along(blocks, dim):
    dims = list(blocks.shape[1:])
    dims[dim] *= blocks.shape[0]
    return jnp.moveaxis(blocks, 0, dim).reshape(dims)


def one_gather(arrays, axis, dims):
    vector = jnp.concatenate([a.reshape(-1) for a in arrays])
    lines, at, finished = (lax.all_gather(vector, axis), 0, [])
    for a, dim in zip(arrays, dims):
        blocks = lines[:, at : at + a.size].reshape(-1, *a.shape)
        finished.append(joined_along(blocks, dim))
        at += a.size
    return tuple(finished)


def copy_for_each(array, axis):
    copies = jnp.broadcast_to(array, (lax.axis_size(axis), *array.shape))
    return lax.all_to_all(copies, axis, split_axis=0, concat_axis=0, tiled=True)


def collect(array, axis, dim):
    blocks = copy_for_each(array, axis)
    return joined_along(blocks, dim)


def lateral(features, weight, offset):
    images, rows, columns, channels = features.shape
    summed = (
        jnp.dot(features.reshape(-1, channels), weight, preferred_element_type=jnp.float32) + offset
    )
    return summed.reshape(images, rows, columns, -1)


def enlarge(coarse):
    return jnp.repeat(jnp.repeat(coarse, 2, axis=1), 2, axis=2)


def conv_rows(padded, weight, offset):
    images, rows_in, columns, channels = padded.shape
    height = rows_in - 2
    framed = jnp.pad(padded, ((0, 0), (0, 0), (1, 1), (0, 0)))
    summed = jnp.zeros((images * height * columns, weight.shape[3]), jnp.float32)
    for row_off in range(3):
        for col_off in range(3):
            window = framed[:, row_off : row_off + height, col_off : col_off + columns, :].reshape(
                -1, channels
            )
            summed = summed + jnp.dot(
                window, weight[row_off, col_off], preferred_element_type=jnp.float32
            )
    return (summed + offset).reshape(images, height, columns, -1).astype(jnp.bfloat16)


def joined_rims(fields):
    images = fields[0].shape[0]
    firsts = jnp.concatenate([field[:, 0].reshape(images, -1) for field in fields], axis=1)
    lasts = jnp.concatenate([field[:, -1].reshape(images, -1) for field in fields], axis=1)
    above = shifted(lasts, "space", 1)
    below = shifted(firsts, "space", -1)
    rimmed = []
    start = 0
    for field in fields:
        width = field.shape[2] * field.shape[3]
        upper = above[:, start : start + width].reshape(images, 1, field.shape[2], field.shape[3])
        lower = below[:, start : start + width].reshape(images, 1, field.shape[2], field.shape[3])
        rimmed.append(jnp.concatenate([upper, field, lower], axis=1))
        start = start + width
    return rimmed


def on_device(
    section_three,
    section_four,
    section_five,
    lateral_three,
    lateral_four,
    lateral_five,
    lateral_bias_three,
    lateral_bias_four,
    lateral_bias_five,
    output_three,
    output_four,
    output_five,
    output_bias_three,
    output_bias_four,
    output_bias_five,
):
    whole_lat3, whole_lat4, whole_lat5, whole_out3, whole_out4, whole_out5 = one_gather(
        (lateral_three, lateral_four, lateral_five, output_three, output_four, output_five),
        "space",
        (0, 0, 0, 2, 2, 2),
    )
    merged_five = lateral(section_five, whole_lat5, lateral_bias_five).astype(jnp.bfloat16)
    merged_four = (
        lateral(section_four, whole_lat4, lateral_bias_four)
        + enlarge(merged_five).astype(jnp.float32)
    ).astype(jnp.bfloat16)
    merged_three = (
        lateral(section_three, whole_lat3, lateral_bias_three)
        + enlarge(merged_four).astype(jnp.float32)
    ).astype(jnp.bfloat16)
    rimmed_three, rimmed_four = joined_rims([merged_three, merged_four])
    level_three = conv_rows(rimmed_three, whole_out3, output_bias_three)
    level_four = conv_rows(rimmed_four, whole_out4, output_bias_four)
    whole_five = collect(merged_five, "space", 1)
    padded_five = jnp.pad(whole_five, ((0, 0), (1, 1), (0, 0), (0, 0)))
    level_five = conv_rows(padded_five, whole_out5, output_bias_five)
    level_six = level_five[:, ::2, ::2, :]
    return (level_three, level_four, level_five, level_six)


def solution(mesh):
    return jax.shard_map(
        on_device,
        mesh=mesh,
        in_specs=(
            P("dp", "space", None, None),
            P("dp", "space", None, None),
            P("dp", "space", None, None),
            P("space", None),
            P("space", None),
            P("space", None),
            P(),
            P(),
            P(),
            P(None, None, "space", None),
            P(None, None, "space", None),
            P(None, None, "space", None),
            P(),
            P(),
            P(),
        ),
        out_specs=(
            P("dp", "space", None, None),
            P("dp", "space", None, None),
            P("dp", None, None, None),
            P("dp", None, None, None),
        ),
        check_vma=False,
    )
```

profile of v0, /device:TPU:1, one launch (start us, length us, event | category | flops | bytes accessed | tf_op | source)
XLA Modules:
  0.0 228.3 jit_solution(411189829314723275)
XLA Ops:
  9.7 0.9 copy.70
  10.7 0.9 copy.71
  11.6 0.9 copy.72
  13.4 129.0 %all-gather.3.cloned.1.call-done = bf16[2686976]{0:T(1024)(128)(2,1)} async-done(((bf16[167936]{0:T(1024)(128)(2,1)}), bf16[2686976]{0:T(1024)(128)(2,1)}) %all-gather.3.cloned.1.call-update) | async-done | bytes 5373968 | tf_op jit(solution)/shard_map/all_gather | solution.py:21
  142.4 5.6 %reshape.343 = bf16[16,167936]{1,0:T(8,128)(2,1)} reshape(bf16[2686976]{0:T(1024)(128)(2,1)} %all-gather.3.cloned.1.call-done) | data formatting | bytes 10747904 | tf_op jit(solution)/shard_map/all_gather | solution.py:21
  148.0 3.7 %fusion.28 = (bf16[16,36864]{1,0:T(8,128)(2,1)}, bf16[16,36864]{1,0:T(8,128)(2,1)S(1)}, bf16[16,36864]{1,0:T(8,128)(2,1)}) fusion(bf16[16,167936]{1,0:T(8,128)(2,1)} %reshape.343), kind=kLoop, calls=%fused_computation.113 | loop fusion | bytes 7077888 | tf_op jit(solution)/shard_map/slice | solution.py:23
  151.7 1.4 reshape_reshape.11
  153.1 1.6 fusion.10
  155.7 0.9 convert_element_type.158
  157.4 1.0 reshape_reshape.10
  158.4 1.4 convolution_add_fusion.16
  160.1 1.5 copy.48
  161.6 1.6 convolution_add_fusion.25
  165.4 1.4 fusion.13
  167.9 1.3 collective-permute-start.1
  170.9 1.0 copy.66
  171.9 1.5 copy.78
  173.4 1.1 copy.65
  174.9 4.7 %collective-permute-start = (bf16[1,49152]{1,0:T(2,128)(2,1)}, bf16[1,49152]{1,0:T(2,128)(2,1)}, u32[]{:S(2)}, u32[]{:S(2)}) collective-permute-start(bf16[1,49152]{1,0:T(2,128)(2,1)} %pad_maximum_fusion.2), channel_id=1, source_target_pairs={{0,1},{1,2},{2,3},{3,4},{4,5},{5,6},{6,7},{7,8},{8,9},{9,10},{10,1... | collective-permute-start | bytes 294920 | tf_op jit(solution)/shard_map/ppermute | solution.py:10
  180.4 5.2 %all-to-all-start = ((bf16[16,1,2,32,256]{4,3,2,1,0:T(8,128)(2,1)}), bf16[16,1,2,32,256]{4,3,2,1,0:T(8,128)(2,1)S(1)}, u32[]{:S(2)}, u32[]{:S(2)}) async-start(bf16[16,1,2,32,256]{4,3,2,1,0:T(8,128)(2,1)} %broadcast_in_dim.25), calls=%async_computation | async-start | bytes 1048576 | tf_op jit(solution)/shard_map/all_to_all | solution.py:31
  185.6 2.4 %broadcast_in_dim.24.clone = f32[8,64,2,256]{3,2,1,0:T(2,128)} broadcast(f32[8,64,256]{2,1,0:T(8,128)} %copy.66), dimensions={0,1,3} | broadcast | bytes 1572864 | tf_op jit(solution)/shard_map/broadcast_in_dim | solution.py:48
  188.0 2.9 %convert_element_type.166 = f32[1024,256]{1,0:T(8,128)} reshape(f32[8,64,2,256]{3,2,1,0:T(2,128)} %broadcast_in_dim.24.clone) | data formatting | bytes 2097152 | tf_op jit(solution)/shard_map/convert_element_type | solution.py:113
  190.9 2.5 %copy.58 = f32[1024,256]{0,1:T(8,128)} copy(f32[1024,256]{1,0:T(8,128)} %convert_element_type.166) | data formatting | bytes 2097152 | tf_op jit(solution)/shard_map/convert_element_type | solution.py:113
  193.5 1.5 copy.76
  195.0 1.1 copy.52
  196.1 1.0 slice_reduce_fusion
  197.2 1.0 slice_reduce_fusion.1
  198.3 1.0 slice.288
  199.4 1.0 slice.285
  206.5 0.9 copy-done.6
  210.7 1.1 fusion.3
  216.4 5.1 %slice.279 = bf16[1,16,16,256]{3,2,1,0:T(8,128)(2,1)} slice(bf16[1,32,32,256]{3,2,1,0:T(8,128)(2,1)S(1)} %bitcast.278), slice={[0:1:1], [0:32:2], [0:32:2], [0:256:1]} | slice | bytes 262144 | tf_op jit(solution)/shard_map/slice | solution.py:121
  (134 shorter events, 25.3 us)
Async XLA Ops:
  7.2 151.3 %copy-start = (bf16[1,8,128,512]{3,2,1,0:T(8,128)(2,1)S(1)}, bf16[1,8,128,512]{3,2,1,0:T(8,128)(2,1)}, u32[]{:S(2)}) copy-start(bf16[1,8,128,512]{3,2,1,0:T(8,128)(2,1)} %param.15) | copy-start | bytes 3145732
  7.2 135.2 %all-gather.3.cloned.1.call-start = ((), (), s32[]{:S(2)}) async-start(), calls=%async_computation.1 | async-start | bytes 5709824 | tf_op jit(solution)/shard_map/all_gather | solution.py:21
  12.7 0.7 copy-start.13
  148.0 3.7 %slice-start.2 = ((bf16[16,167936]{1,0:T(8,128)(2,1)}), bf16[16,32768]{1,0:T(8,128)(2,1)S(1)}, s32[]{:S(2)}) async-start(bf16[16,167936]{1,0:T(8,128)(2,1)} %reshape.343), calls=%async_computation.4 | async-start | bytes 2097152 | tf_op jit(solution)/shard_map/slice | solution.py:23
  151.7 1.4 copy-start.18
  151.7 1.4 copy-start.19
  153.1 3.5 %slice-start = ((bf16[16,167936]{1,0:T(8,128)(2,1)}), bf16[16,8192]{1,0:T(8,128)(2,1)S(1)}, s32[]{:S(2)}) async-start(bf16[16,167936]{1,0:T(8,128)(2,1)} %reshape.343), calls=%async_computation.2 | async-start | bytes 524288 | tf_op jit(solution)/shard_map/slice | solution.py:23
  154.6 3.8 %copy-start.14 = (bf16[256,64]{0,1:T(8,128)(2,1)}, bf16[256,64]{0,1:T(8,128)(2,1)S(1)}, u32[]{:S(2)}) copy-start(bf16[256,64]{0,1:T(8,128)(2,1)S(1)} %fusion.10) | copy-start | bytes 98308
  154.6 2.7 %slice-start.1 = ((bf16[16,167936]{1,0:T(8,128)(2,1)}), bf16[16,16384]{1,0:T(8,128)(2,1)S(1)}, s32[]{:S(2)}) async-start(bf16[16,167936]{1,0:T(8,128)(2,1)} %reshape.343), calls=%async_computation.3 | async-start | bytes 1048576 | tf_op jit(solution)/shard_map/slice | solution.py:23
  155.7 2.8 %copy-start.20 = (f32[256]{0:T(256)S(1)}, f32[256]{0:T(256)}, u32[]{:S(2)}) copy-start(f32[256]{0:T(256)} %param.21) | copy-start | bytes 3076
  160.1 1.5 copy-start.24
  161.6 1.6 copy-start.9
  161.6 1.8 copy-start.10
  163.2 1.7 copy-start.4
  163.5 1.4 copy-start.7
  165.4 1.6 copy-start.17
  165.4 3.8 %copy-start.16 = (bf16[1,1,64,256]{3,1,2,0:T(2,128)(2,1)S(1)}, bf16[1,1,64,256]{3,1,2,0:T(2,128)(2,1)}, u32[]{:S(2)}) copy-start(bf16[1,1,64,256]{3,1,2,0:T(2,128)(2,1)} %copy.74) | copy-start | bytes 98308
  167.9 28.2 %collective-permute-start.1 = (bf16[1,49152]{1,0:T(2,128)(2,1)}, bf16[1,49152]{1,0:T(2,128)(2,1)}, u32[]{:S(2)}, u32[]{:S(2)}) collective-permute-start(bf16[1,49152]{1,0:T(2,128)(2,1)} %pad_maximum_fusion.3), channel_id=1, source_target_pairs={{1,0},{2,1},{3,2},{4,3},{5,4},{6,5},{7,6},{8,7},{9,8},{10,9},{11,1... | collective-permute-start | bytes 294920 | tf_op jit(solution)/shard_map/ppermute | solution.py:10
  174.8 4.8 %copy-start.15 = (bf16[256,64]{0,1:T(8,128)(2,1)S(1)}, bf16[256,64]{0,1:T(8,128)(2,1)}, u32[]{:S(2)}) copy-start(bf16[256,64]{0,1:T(8,128)(2,1)} %copy-done.14) | copy-start | bytes 98308
  174.9 22.3 %collective-permute-start = (bf16[1,49152]{1,0:T(2,128)(2,1)}, bf16[1,49152]{1,0:T(2,128)(2,1)}, u32[]{:S(2)}, u32[]{:S(2)}) collective-permute-start(bf16[1,49152]{1,0:T(2,128)(2,1)} %pad_maximum_fusion.2), channel_id=1, source_target_pairs={{0,1},{1,2},{2,3},{3,4},{4,5},{5,6},{6,7},{7,8},{8,9},{9,10},{10,1... | collective-permute-start | bytes 294920 | tf_op jit(solution)/shard_map/ppermute | solution.py:10
  180.4 31.4 %all-to-all-start = ((bf16[16,1,2,32,256]{4,3,2,1,0:T(8,128)(2,1)}), bf16[16,1,2,32,256]{4,3,2,1,0:T(8,128)(2,1)S(1)}, u32[]{:S(2)}, u32[]{:S(2)}) async-start(bf16[16,1,2,32,256]{4,3,2,1,0:T(8,128)(2,1)} %broadcast_in_dim.25), calls=%async_computation | async-start | bytes 1048576 | tf_op jit(solution)/shard_map/all_to_all | solution.py:31
  195.0 3.2 %copy-start.8 = (bf16[1,4,64,256]{3,2,1,0:T(8,128)(2,1)S(1)}, bf16[1,4,64,256]{3,2,1,0:T(8,128)(2,1)}, u32[]{:S(2)}) copy-start(bf16[1,4,64,256]{3,2,1,0:T(8,128)(2,1)} %copy-done.7) | copy-start | bytes 393220
  202.8 1.0 copy-start.5
  202.8 1.0 copy-start.11
  204.0 1.3 copy-start.2
  206.2 1.2 copy-start.6
  207.9 0.7 copy-start.21
  210.0 0.7 copy-start.22
  212.0 1.3 copy-start.3
  215.4 0.7 copy-start.23
  215.7 5.8 %copy-start.1 = (bf16[1,8,128,512]{3,2,1,0:T(8,128)(2,1)S(1)}, bf16[1,8,128,512]{3,2,1,0:T(8,128)(2,1)}, u32[]{:S(2)}) copy-start(bf16[1,8,128,512]{3,2,1,0:T(8,128)(2,1)} %param.15) | copy-start | bytes 3145732
  216.4 5.1 %copy-start.12 = (bf16[1024,256]{1,0:T(8,128)(2,1)}, bf16[1024,256]{1,0:T(8,128)(2,1)S(1)}, u32[]{:S(2)}) copy-start(bf16[1024,256]{1,0:T(8,128)(2,1)S(1)} %fusion.4) | copy-start | bytes 1572868
Sparse Core Ops, SparseCore 0:
  13.5 128.8 all-gather.2
where the time goes:
time: 230 us; the launch traced here: 228 us
  waiting for transfers between devices  129 us (56%)
  local copies, waits for them, and re-layouts  55.6 us (24%)
  between operations  14.8 us (6%)
  matrix products  13.2 us (6%)
  starting transfers between devices  11.2 us (5%)
  other arithmetic  4.53 us (2%)
    all_gather x1, waiting for transfers between devices, one_gather(): lines, at, finished = (lax.all_gather(vector, axis), 0, [])  129 us
    unnamed x69, local copies, waits for them, and re-layouts  15.7 us
    dot_general x27, matrix products, conv_rows(): jnp.dot(window, weight[row_off, col_off], preferred_element_type=jnp.floa...  8.6 us
    convert_element_type x4, local copies, waits for them, and re-layouts, on_device(): enlarge(merged_four).astype(jnp.float32)  6.02 us
    ppermute x2, starting transfers between devices, shifted(): return lax.ppermute(array, axis, pairs)  5.97 us
    all_gather x1, local copies, waits for them, and re-layouts, one_gather(): lines, at, finished = (lax.all_gather(vector, axis), 0, [])  5.57 us
    all_to_all x1, starting transfers between devices, copy_for_each(): return lax.all_to_all(copies, axis, split_axis=0, concat_axis=0, tiled=True)  5.17 us
    slice x1, local copies, waits for them, and re-layouts, on_device(): level_six = level_five[:, ::2, ::2, :]  5.07 us
  transfers between devices with their start and end apart: 4, of which 1 were waited for; matrix products, arithmetic and copies ran while one was open for 13% of the time, Pallas kernels for 0%

commit v1 on v0

v1 whole, which is shorter than its diff:
```python
import jax
import jax.numpy as jnp
from jax import lax
from jax.experimental import pallas as pl
from jax.experimental.pallas import tpu as pltpu
from jax.sharding import PartitionSpec as P

MESH = pl.DeviceIdType.MESH
BF16 = jnp.bfloat16
F32 = jnp.float32

L5, L4, L3, W5, W3, W4, ROWS = 0, 128, 192, 224, 368, 512, 656
STAGES = ((L5, L4), (L4, W5), (W5, W3), (W3, W4), (W4, ROWS))
PER_STAGE = 12


def half_rows(first, last):
    return first + (((last - first) // 2 + 15) // 16) * 16


def kernel(
    s3, s4, s5, l3, l4, l5, lb3, lb4, lb5, o3, o4, o5, ob3, ob4, ob5,
    out3, out4, out5, out6,
    x3, x4, x5, held, taps, m3, m4, m5, wide4, wide3, even, y3, y4, y5, y6,
    own_sem, load_sem, send, recv, m_send, m_recv, store_sem,
):
    dp, sp = lax.axis_index("dp"), lax.axis_index("space")
    core, x, z_hi = lax.rem(dp, 2), lax.rem(dp // 2, 4), dp // 8
    y, z = sp // 4, lax.rem(sp, 4)

    def pick(for_zero, for_one):
        return for_zero + core * (for_one - for_zero)

    def along_z(by):
        full = lax.rem(z_hi * 4 + z + by + 8, 8)
        return (full // 4) * 8 + x * 2 + core, y * 4 + lax.rem(full, 4)

    def along_y(by):
        return dp, lax.rem(y + by + 4, 4) * 4 + z

    def first_axis(by):
        for_z, for_y = along_z(by), along_y(by)
        return pick(for_z[0], for_y[0]), pick(for_z[1], for_y[1])

    def second_axis(by):
        for_z, for_y = along_z(by), along_y(by)
        return pick(for_y[0], for_z[0]), pick(for_y[1], for_z[1])

    sibling = (dp + 1 - 2 * core, sp)
    a, b = pick(z, y), pick(y, z)
    sib_b = pick(z, y)
    below, above = (dp, lax.rem(sp + 1, 16)), (dp, lax.rem(sp + 15, 16))
    in_line = [(dp, y * 4 + lax.rem(z + i, 4)) for i in (1, 2, 3)]

    own_slot = 4 * b + a
    lanes = pl.ds(pl.multiple_of(core * 128, 128), 128)
    own_loads = []
    for i, (ref, first) in enumerate(((l5, L5), (l4, L4), (l3, L3), (o5, W5), (o3, W3), (o4, W4))):
        count = ref.shape[0]
        own_loads.append(
            pltpu.make_async_copy(
                ref.at[:, lanes], held.at[core, own_slot, first : first + count, :], own_sem.at[i]
            )
        )
    section_loads = [
        pltpu.make_async_copy(ref.at[0], to, load_sem.at[i])
        for i, (ref, to) in enumerate(((s5, x5), (s4, x4), (s3, x3)))
    ]
    for copy in own_loads + section_loads:
        copy.start()
    own_of_stage = ((0,), (1, 2), (3,), (4,), (5,))

    partners = [along_z(1), along_z(-1), along_y(1), along_y(-1), sibling, below, above] + in_line
    barrier = pltpu.get_barrier_semaphore()
    for where in partners:
        pl.semaphore_signal(barrier, inc=1, device_id=where, device_id_type=MESH)

    m5[0] = jnp.zeros_like(m5[0])
    m5[33] = jnp.zeros_like(m5[33])

    pl.semaphore_wait(barrier, len(partners))

    sent = []

    def go(ref, where, stage, index):
        copy = pltpu.make_async_remote_copy(
            src_ref=ref,
            dst_ref=ref,
            send_sem=send.at[stage * PER_STAGE + index],
            recv_sem=recv.at[stage * PER_STAGE + index],
            device_id=where,
            device_id_type=MESH,
        )
        copy.start()
        sent.append(copy)

    def arrived(ref, stage, index):
        pltpu.make_async_remote_copy(
            src_ref=ref,
            dst_ref=ref,
            send_sem=send.at[stage * PER_STAGE + index],
            recv_sem=recv.at[stage * PER_STAGE + index],
            device_id=sibling,
            device_id_type=MESH,
        ).wait_recv()

    def slot(by, first, last):
        return held.at[core, 4 * b + lax.rem(a + by, 4), first:last, :]

    def block(by, first, last, at=0, count=4):
        return held.at[core, pl.ds(4 * lax.rem(b + by, 4) + at, count), first:last, :]

    def step(stage, k):
        first, last = STAGES[stage]
        mid = half_rows(first, last)
        if k == 0:
            for i in own_of_stage[stage]:
                own_loads[i].wait()
            go(slot(0, first, last), first_axis(1), stage, 0)
            go(slot(0, first, last), first_axis(-1), stage, 1)
        elif k == 1:
            arrived(slot(3, first, last), stage, 0)
            go(slot(3, first, mid), first_axis(1), stage, 2)
            arrived(slot(1, first, last), stage, 1)
            go(slot(1, mid, last), first_axis(-1), stage, 3)
        elif k == 2:
            arrived(slot(2, first, mid), stage, 2)
            arrived(slot(2, mid, last), stage, 3)
            go(block(0, first, last), second_axis(1), stage, 4)
            go(block(0, first, last), second_axis(-1), stage, 5)
            go(block(0, first, last), sibling, stage, 8)
        elif k == 3:
            arrived(block(3, first, last), stage, 4)
            go(block(3, first, last, 0, 2), second_axis(1), stage, 6)
            arrived(block(1, first, last), stage, 5)
            go(block(1, first, last, 2, 2), second_axis(-1), stage, 7)
            go(block(3, first, last), sibling, stage, 9)
            go(block(1, first, last), sibling, stage, 10)
        elif k == 4:
            arrived(block(2, first, last, 0, 2), stage, 6)
            arrived(block(2, first, last, 2, 2), stage, 7)
            go(block(2, first, last), sibling, stage, 11)
        else:
            for by, index in ((0, 8), (3, 9), (1, 10), (2, 11)):
                at = 4 * lax.rem(sib_b + by, 4)
                arrived(held.at[1 - core, pl.ds(at, 4), first:last, :], stage, index)

    def weights(first, count, chunks):
        left = jnp.concatenate([held[0, s, first : first + count, :] for s in chunks], axis=0)
        right = jnp.concatenate(
            [held[1, 4 * (s % 4) + s // 4, first : first + count, :] for s in chunks], axis=0
        )
        return jnp.concatenate([left, right], axis=1)

    def lateral(features, first, count):
        per = 256 // count
        total = None
        for start in range(0, 16, per):
            term = jnp.dot(
                features[:, start * count : (start + per) * count],
                weights(first, count, range(start, start + per)),
                preferred_element_type=F32,
            )
            total = term if total is None else total + term
        return total

    def doubled(field, ref):
        count = field.shape[0]
        for h in range(2):
            for odd in range(2):
                ref[h, pl.ds(odd, count, 2), :] = field[:, 128 * h : 128 * h + 128]

    def doubled_rows(ref, first, count):
        return jnp.concatenate([ref[h, first : first + count, :] for h in range(2)], axis=1)

    m_sent = []

    def m_copy(ref, to, where, index):
        return pltpu.make_async_remote_copy(
            src_ref=ref,
            dst_ref=to,
            send_sem=m_send.at[index],
            recv_sem=m_recv.at[index],
            device_id=where,
            device_id_type=MESH,
        )

    def m_go(ref, to, where, index):
        copy = m_copy(ref, to, where, index)
        copy.start()
        m_sent.append(copy)

    def rows5(first, count):
        return m5.at[pl.ds(1 + first, count)]

    def merge_five():
        section_loads[0].wait()
        merged = lateral(x5[...].reshape(64, 2048), L5, 128) + lb5[...]
        rounded = merged.astype(BF16)
        m5[pl.ds(1 + 2 * sp, 2)] = rounded.reshape(2, 32, 256)
        doubled(rounded.astype(F32), wide4)
        for i in (1, 2, 3):
            m_go(rows5(2 * sp, 2), rows5(2 * sp, 2), in_line[i - 1], i - 1)

    def line_done():
        for i in (1, 2, 3):
            ref = rows5(8 * y + 2 * lax.rem(z + 4 - i, 4), 2)
            m_copy(ref, ref, in_line[0], i - 1).wait_recv()
        ref = rows5(8 * y, 8)
        m_go(ref, ref, along_y(1), 3)
        m_go(ref, ref, along_y(-1), 4)

    def column_done():
        left, right = 8 * lax.rem(y + 3, 4), 8 * lax.rem(y + 1, 4)
        m_copy(rows5(left, 8), rows5(left, 8), along_y(1), 3).wait_recv()
        m_go(rows5(left, 4), rows5(left, 4), along_y(1), 5)
        m_copy(rows5(right, 8), rows5(right, 8), along_y(1), 4).wait_recv()
        m_go(rows5(right + 4, 4), rows5(right + 4, 4), along_y(-1), 6)

    def all_five():
        far = 8 * lax.rem(y + 2, 4)
        m_copy(rows5(far, 4), rows5(far, 4), along_y(1), 5).wait_recv()
        m_copy(rows5(far + 4, 4), rows5(far + 4, 4), along_y(1), 6).wait_recv()

    def merge_four_and_three():
        section_loads[1].wait()
        up = jnp.concatenate([doubled_rows(wide4, 64 * (r // 2), 64) for r in range(4)], axis=0)
        merged = lateral(x4[...].reshape(256, 1024), L4, 64) + lb4[...] + up
        rounded = merged.astype(BF16)
        m4[1:5] = rounded.reshape(4, 64, 256)
        m_go(m4.at[4:5], m4.at[0:1], below, 7)
        m_go(m4.at[1:2], m4.at[5:6], above, 8)
        doubled(rounded.astype(F32), wide3)
        section_loads[2].wait()
        for r in (0, 3, 1, 2):
            up = doubled_rows(wide3, 128 * r, 128)
            merged = lateral(x3[2 * r : 2 * r + 2].reshape(256, 512), L3, 32) + lb3[...]
            merged = merged + jnp.concatenate([up, up], axis=0)
            m3[1 + 2 * r : 3 + 2 * r] = merged.astype(BF16).reshape(2, 128, 256)
        m_go(m3.at[8:9], m3.at[0:1], below, 9)
        m_go(m3.at[1:2], m3.at[9:10], above, 10)

    def rims(ref, index, last):
        m_copy(ref.at[0:1], ref.at[0:1], below, index).wait_recv()
        m_copy(ref.at[last : last + 1], ref.at[last : last + 1], below, index + 1).wait_recv()

        @pl.when(sp == 0)
        def _():
            ref[0] = jnp.zeros_like(ref[0])

        @pl.when(sp == 15)
        def _():
            ref[last] = jnp.zeros_like(ref[last])

    def conv(ref, rows, columns, first, offset, each, keep):
        for c in range(3):
            for r in range(3):
                taps[c, 256 * r : 256 * r + 256, :] = weights(first + 16 * (3 * r + c), 16, range(16))
        count = each * columns
        column = lax.rem(lax.broadcasted_iota(jnp.int32, (count, 256), 0), columns)
        for start in range(0, rows, each):
            window = jnp.concatenate(
                [ref[start + r : start + r + each].reshape(count, 256) for r in range(3)], axis=1
            )
            parts = [jnp.dot(window, taps[c], preferred_element_type=F32) for c in range(3)]
            left = jnp.where(column == 0, 0.0, pltpu.roll(parts[0], 1, 0))
            right = jnp.where(column == columns - 1, 0.0, pltpu.roll(parts[2], count - 1, 0))
            summed = parts[1] + offset[...] + left + right
            keep(start, summed.astype(BF16).reshape(each, columns, 256))

    stores = []

    def store(ref, to):
        copy = pltpu.make_async_copy(ref, to, store_sem.at[len(stores)])
        copy.start()
        stores.append(copy)

    def keep5(start, rounded):
        y5[start : start + 8] = rounded
        store(y5.at[start : start + 8], out5.at[0, start : start + 8])
        for r in range(0, 8, 2):
            for h in range(2):
                even[h, 16 * r : 16 * r + 32, :] = rounded[r, :, 128 * h : 128 * h + 128].astype(F32)
        for h in range(2):
            picked = even[h, pl.ds(0, 64, 2), :].astype(BF16).reshape(4, 16, 128)
            y6[start // 2 : start // 2 + 4, :, 128 * h : 128 * h + 128] = picked

    def keep3(start, rounded):
        y3[start : start + 2] = rounded
        store(y3.at[start : start + 2], out3.at[0, start : start + 2])

    def keep4(start, rounded):
        y4[start : start + 4] = rounded
        store(y4.at[start : start + 4], out4.at[0, start : start + 4])

    for slot_of_time in range(9):
        for stage in range(5):
            k = slot_of_time - stage
            if 0 <= k <= 5:
                step(stage, k)
                if k == 5 and stage == 0:
                    merge_five()
                if k == 5 and stage == 1:
                    merge_four_and_three()
                    line_done()
                if k == 5 and stage == 2:
                    column_done()
                if k == 5 and stage == 3:
                    all_five()
                    conv(m5, 32, 32, W5, ob5, 8, keep5)
                    store(y6, out6.at[0])
    rims(m3, 9, 9)
    conv(m3, 8, 128, W3, ob3, 2, keep3)
    step(4, 5)
    rims(m4, 7, 5)
    conv(m4, 4, 64, W4, ob4, 4, keep4)
    for copy in sent + m_sent:
        copy.wait_send()
    for copy in stores:
        copy.wait()


def on_device(
    section_three,
    section_four,
    section_five,
    lateral_three,
    lateral_four,
    lateral_five,
    lateral_bias_three,
    lateral_bias_four,
    lateral_bias_five,
    output_three,
    output_four,
    output_five,
    output_bias_three,
    output_bias_four,
    output_bias_five,
):
    anywhere = pl.BlockSpec(memory_space=pl.ANY)
    in_vmem = pl.BlockSpec(memory_space=pltpu.VMEM)
    row = [bias.reshape(1, 256) for bias in (
        lateral_bias_three, lateral_bias_four, lateral_bias_five,
        output_bias_three, output_bias_four, output_bias_five)]
    dma = pltpu.SemaphoreType.DMA
    return pl.pallas_call(
        kernel,
        out_shape=(
            jax.ShapeDtypeStruct((1, 8, 128, 256), BF16),
            jax.ShapeDtypeStruct((1, 4, 64, 256), BF16),
            jax.ShapeDtypeStruct((1, 32, 32, 256), BF16),
            jax.ShapeDtypeStruct((1, 16, 16, 256), BF16),
        ),
        in_specs=[anywhere] * 6 + [in_vmem] * 3 + [anywhere] * 3 + [in_vmem] * 3,
        out_specs=(anywhere,) * 4,
        scratch_shapes=[
            pltpu.VMEM((8, 128, 512), BF16),
            pltpu.VMEM((4, 64, 1024), BF16),
            pltpu.VMEM((2, 32, 2048), BF16),
            pltpu.VMEM((2, 16, ROWS, 128), BF16),
            pltpu.VMEM((3, 768, 256), BF16),
            pltpu.VMEM((10, 128, 256), BF16),
            pltpu.VMEM((6, 64, 256), BF16),
            pltpu.VMEM((34, 32, 256), BF16),
            pltpu.VMEM((2, 128, 128), F32),
            pltpu.VMEM((2, 512, 128), F32),
            pltpu.VMEM((2, 128, 128), F32),
            pltpu.VMEM((8, 128, 256), BF16),
            pltpu.VMEM((4, 64, 256), BF16),
            pltpu.VMEM((32, 32, 256), BF16),
            pltpu.VMEM((16, 16, 256), BF16),
            dma((6,)),
            dma((3,)),
            dma((len(STAGES) * PER_STAGE,)),
            dma((len(STAGES) * PER_STAGE,)),
            dma((11,)),
            dma((11,)),
            dma((10,)),
        ],
        compiler_params=pltpu.CompilerParams(
            collective_id=0, has_side_effects=True, vmem_limit_bytes=40 * 1024 * 1024
        ),
    )(
        section_three, section_four, section_five,
        lateral_three, lateral_four, lateral_five, row[0], row[1], row[2],
        output_three.reshape(144, 256), output_four.reshape(144, 256),
        output_five.reshape(144, 256), row[3], row[4], row[5],
    )


def solution(mesh):
    return jax.shard_map(
        on_device,
        mesh=mesh,
        in_specs=(
            P("dp", "space", None, None),
            P("dp", "space", None, None),
            P("dp", "space", None, None),
            P("space", None),
            P("space", None),
            P("space", None),
            P(),
            P(),
            P(),
            P(None, None, "space", None),
            P(None, None, "space", None),
            P(None, None, "space", None),
            P(),
            P(),
            P(),
        ),
        out_specs=(
            P("dp", "space", None, None),
            P("dp", "space", None, None),
            P("dp", None, None, None),
            P("dp", None, None, None),
        ),
        check_vma=False,
    )
```

time: 230 us -> 67.4 us (0.29)
  waiting for transfers between devices: 129 us -> 0 us
  Pallas kernels: 0 us -> 51.7 us
  local copies, waits for them, and re-layouts: 55.6 us -> 14.5 us
  between operations: 14.8 us -> 0.68 us
  matrix products: 13.2 us -> 0 us
  starting transfers between devices: 11.2 us -> 0 us
  other arithmetic: 4.53 us -> 0 us
    all_gather x1 -> x0, waiting for transfers between devices: 129 us -> none  [one_gather(): lines, at, finished = (lax.all_gather(vector, axis), 0, [])]
    pallas_call x0 -> x1, Pallas kernels: none -> 51.7 us  [on_device(): pl.pallas_call(kernel, out_shape=(jax.ShapeDtypeStruct((1, 8, 128, 256),...]
    slice x25 -> x0, local copies, waits for them, and re-layouts: 15 us -> none  [the longest x1 5.07 us: on_device(): level_six = level_five[:, ::2, ::2, :]]
    dot_general x30 -> x0, matrix products: 13.2 us -> none  [the longest x27 8.6 us: conv_rows(): jnp.dot(window, weight[row_off, col_off], preferred_element_type=jnp.floa...]
    convert_element_type x7 -> x0, local copies, waits for them, and re-layouts: 8.69 us -> none  [the longest x4 6.02 us: on_device(): enlarge(merged_four).astype(jnp.float32)]
    ppermute x2 -> x0, starting transfers between devices: 5.97 us -> none  [shifted(): return lax.ppermute(array, axis, pairs)]
    all_gather x1 -> x0, local copies, waits for them, and re-layouts: 5.57 us -> none  [one_gather(): lines, at, finished = (lax.all_gather(vector, axis), 0, [])]
    all_to_all x1 -> x0, starting transfers between devices: 5.17 us -> none  [copy_for_each(): return lax.all_to_all(copies, axis, split_axis=0, concat_axis=0, tiled=True)]
  transfers between devices with their start and end apart: 4 -> 0, of which waited for: 1 -> 0; matrix products, arithmetic and copies ran while one was open for 13% -> 0% of each run, Pallas kernels for 0% -> 0%
where the time goes in v1:
time: 67.4 us; the launch traced here: 66.8 us
  Pallas kernels  51.7 us (77%)
  local copies, waits for them, and re-layouts  14.5 us (22%)
  between operations  0.68 us (1%)
    pallas_call x1, Pallas kernels, on_device(): pl.pallas_call(kernel, out_shape=(jax.ShapeDtypeStruct((1, 8, 128, 256),...  51.7 us
    unnamed x34, local copies, waits for them, and re-layouts  14.5 us

profile of v1, /device:TPU:1, one launch (start us, length us, event | category | flops | bytes accessed | tf_op | source)
XLA Modules:
  0.0 66.8 jit_solution(17560363471183537145)
XLA Ops:
  0.6 0.0 copy-start.8
  0.6 0.0 copy-start.9
  0.7 0.7 %copy-done.8 = bf16[32,256]{1,0:T(8,128)(2,1)S(1)} copy-done((bf16[32,256]{1,0:T(8,128)(2,1)S(1)}, bf16[32,256]{1,0:T(8,128)(2,1)}, u32[]{:S(2)}) %copy-start.8) | copy-done | bytes 16408
  1.4 0.0 copy-done.9
  1.4 0.0 copy-start
  1.4 1.2 %copy-done = bf16[1,8,128,512]{3,2,1,0:T(8,128)(2,1)S(1)} copy-done((bf16[1,8,128,512]{3,2,1,0:T(8,128)(2,1)S(1)}, bf16[1,8,128,512]{3,2,1,0:T(8,128)(2,1)}, u32[]{:S(2)}) %copy-start) | copy-done | bytes 1048600
  2.6 0.0 copy-start.1
  2.6 1.0 %copy-done.1 = bf16[1,4,64,1024]{3,2,1,0:T(8,128)(2,1)S(1)} copy-done((bf16[1,4,64,1024]{3,2,1,0:T(8,128)(2,1)S(1)}, bf16[1,4,64,1024]{3,2,1,0:T(8,128)(2,1)}, u32[]{:S(2)}) %copy-start.1) | copy-done | bytes 524312
  3.6 0.0 copy-start.2
  3.6 0.9 %copy-done.2 = bf16[1,2,32,2048]{3,2,1,0:T(8,128)(2,1)S(1)} copy-done((bf16[1,2,32,2048]{3,2,1,0:T(8,128)(2,1)S(1)}, bf16[1,2,32,2048]{3,2,1,0:T(8,128)(2,1)}, u32[]{:S(2)}) %copy-start.2) | copy-done | bytes 262168
  4.6 0.0 copy-start.3
  4.6 0.9 %copy-done.3 = bf16[3,3,16,256]{3,2,1,0:T(8,128)(2,1)S(1)} copy-done((bf16[3,3,16,256]{3,2,1,0:T(8,128)(2,1)S(1)}, bf16[3,3,16,256]{3,2,1,0:T(8,128)(2,1)}, u32[]{:S(2)}) %copy-start.3) | copy-done | bytes 73752
  5.5 0.0 copy-start.4
  5.5 0.9 %copy-done.4 = bf16[3,3,16,256]{3,2,1,0:T(8,128)(2,1)S(1)} copy-done((bf16[3,3,16,256]{3,2,1,0:T(8,128)(2,1)S(1)}, bf16[3,3,16,256]{3,2,1,0:T(8,128)(2,1)}, u32[]{:S(2)}) %copy-start.4) | copy-done | bytes 73752
  6.3 0.0 copy-start.5
  6.3 0.9 %copy-done.5 = bf16[3,3,16,256]{3,2,1,0:T(8,128)(2,1)S(1)} copy-done((bf16[3,3,16,256]{3,2,1,0:T(8,128)(2,1)S(1)}, bf16[3,3,16,256]{3,2,1,0:T(8,128)(2,1)}, u32[]{:S(2)}) %copy-start.5) | copy-done | bytes 73752
  7.2 0.0 copy-start.6
  7.2 0.8 %copy-done.6 = bf16[128,256]{1,0:T(8,128)(2,1)S(1)} copy-done((bf16[128,256]{1,0:T(8,128)(2,1)S(1)}, bf16[128,256]{1,0:T(8,128)(2,1)}, u32[]{:S(2)}) %copy-start.6) | copy-done | bytes 65560
  8.1 0.0 copy-start.7
  8.1 0.8 %copy-done.7 = bf16[64,256]{1,0:T(8,128)(2,1)S(1)} copy-done((bf16[64,256]{1,0:T(8,128)(2,1)S(1)}, bf16[64,256]{1,0:T(8,128)(2,1)}, u32[]{:S(2)}) %copy-start.7) | copy-done | bytes 32792
  8.8 0.0 copy-start.10
  8.8 0.7 %copy-done.10 = f32[256]{0:T(256)S(1)} copy-done((f32[256]{0:T(256)S(1)}, f32[256]{0:T(256)}, u32[]{:S(2)}) %copy-start.10) | copy-done | bytes 1048
  9.5 0.0 copy-start.11
  9.5 0.7 %copy-done.11 = f32[256]{0:T(256)S(1)} copy-done((f32[256]{0:T(256)S(1)}, f32[256]{0:T(256)}, u32[]{:S(2)}) %copy-start.11) | copy-done | bytes 1048
  10.2 0.7 %copy-done.12 = f32[256]{0:T(256)S(1)} copy-done((f32[256]{0:T(256)S(1)}, f32[256]{0:T(256)}, u32[]{:S(2)}) %copy-start.12) | copy-done | bytes 1048
  10.9 0.7 %copy-done.13 = f32[256]{0:T(256)S(1)} copy-done((f32[256]{0:T(256)S(1)}, f32[256]{0:T(256)}, u32[]{:S(2)}) %copy-start.13) | copy-done | bytes 1048
  11.5 0.7 %copy-done.14 = f32[256]{0:T(256)S(1)} copy-done((f32[256]{0:T(256)S(1)}, f32[256]{0:T(256)}, u32[]{:S(2)}) %copy-start.14) | copy-done | bytes 1048
  12.2 51.7 %shard_map.174 = (bf16[1,8,128,256]{3,2,1,0:T(8,128)(2,1)S(1)}, bf16[1,4,64,256]{3,2,1,0:T(8,128)(2,1)S(1)}, bf16[1,32,32,256]{3,2,1,0:T(8,128)(2,1)S(1)}, bf16[1,16,16,256]{3,2,1,0:T(8,128)(2,1)S(1)}) custom-call(bf16[1,8,128,512]{3,2,1,0:T(8,128)(2,1)S(1)} %copy-done, bf16[1,4,64,1024]{3,2,1,0:T(8,128)(2,1)S(1)} %copy-done.1, ...), custom_call_target="tpu_custom_call" | custom-call | tf_op jit(solution)/shard_map/pallas_call | solution.py:346
  63.9 0.8 %copy.23 = bf16[1,8,128,256]{3,2,1,0:T(8,128)(2,1)} copy(bf16[1,8,128,256]{3,2,1,0:T(8,128)(2,1)S(1)} %get-tuple-element.8) | data formatting | bytes 1048576
  64.7 0.7 copy.24
  65.4 0.8 %copy.25 = bf16[1,32,32,256]{3,2,1,0:T(8,128)(2,1)} copy(bf16[1,32,32,256]{3,2,1,0:T(8,128)(2,1)S(1)} %get-tuple-element.10) | data formatting | bytes 1048576
  66.2 0.7 copy.26
  (3 shorter events, 0.0 us)
Async XLA Ops:
  0.6 0.7 %copy-start.8 = (bf16[32,256]{1,0:T(8,128)(2,1)S(1)}, bf16[32,256]{1,0:T(8,128)(2,1)}, u32[]{:S(2)}) copy-start(bf16[32,256]{1,0:T(8,128)(2,1)} %l3.1) | copy-start | bytes 49156
  0.6 0.7 %copy-start.9 = (f32[256]{0:T(256)S(1)}, f32[256]{0:T(256)}, u32[]{:S(2)}) copy-start(f32[256]{0:T(256)} %param.21) | copy-start | bytes 3076
  1.4 1.2 %copy-start = (bf16[1,8,128,512]{3,2,1,0:T(8,128)(2,1)S(1)}, bf16[1,8,128,512]{3,2,1,0:T(8,128)(2,1)}, u32[]{:S(2)}) copy-start(bf16[1,8,128,512]{3,2,1,0:T(8,128)(2,1)} %s3.1) | copy-start | bytes 3145732
  2.6 1.0 %copy-start.1 = (bf16[1,4,64,1024]{3,2,1,0:T(8,128)(2,1)S(1)}, bf16[1,4,64,1024]{3,2,1,0:T(8,128)(2,1)}, u32[]{:S(2)}) copy-start(bf16[1,4,64,1024]{3,2,1,0:T(8,128)(2,1)} %s4_.1) | copy-start | bytes 1572868
  3.6 0.9 %copy-start.2 = (bf16[1,2,32,2048]{3,2,1,0:T(8,128)(2,1)S(1)}, bf16[1,2,32,2048]{3,2,1,0:T(8,128)(2,1)}, u32[]{:S(2)}) copy-start(bf16[1,2,32,2048]{3,2,1,0:T(8,128)(2,1)} %s5.1) | copy-start | bytes 786436
  4.6 0.9 %copy-start.3 = (bf16[3,3,16,256]{3,2,1,0:T(8,128)(2,1)S(1)}, bf16[3,3,16,256]{3,2,1,0:T(8,128)(2,1)}, u32[]{:S(2)}) copy-start(bf16[3,3,16,256]{3,2,1,0:T(8,128)(2,1)} %param.24) | copy-start | bytes 221188
  5.5 0.9 %copy-start.4 = (bf16[3,3,16,256]{3,2,1,0:T(8,128)(2,1)S(1)}, bf16[3,3,16,256]{3,2,1,0:T(8,128)(2,1)}, u32[]{:S(2)}) copy-start(bf16[3,3,16,256]{3,2,1,0:T(8,128)(2,1)} %param.25) | copy-start | bytes 221188
  6.3 0.9 %copy-start.5 = (bf16[3,3,16,256]{3,2,1,0:T(8,128)(2,1)S(1)}, bf16[3,3,16,256]{3,2,1,0:T(8,128)(2,1)}, u32[]{:S(2)}) copy-start(bf16[3,3,16,256]{3,2,1,0:T(8,128)(2,1)} %param.26) | copy-start | bytes 221188
  7.2 0.8 %copy-start.6 = (bf16[128,256]{1,0:T(8,128)(2,1)S(1)}, bf16[128,256]{1,0:T(8,128)(2,1)}, u32[]{:S(2)}) copy-start(bf16[128,256]{1,0:T(8,128)(2,1)} %l5.1) | copy-start | bytes 196612
  8.1 0.8 %copy-start.7 = (bf16[64,256]{1,0:T(8,128)(2,1)S(1)}, bf16[64,256]{1,0:T(8,128)(2,1)}, u32[]{:S(2)}) copy-start(bf16[64,256]{1,0:T(8,128)(2,1)} %l4.1) | copy-start | bytes 98308
  8.8 0.7 %copy-start.10 = (f32[256]{0:T(256)S(1)}, f32[256]{0:T(256)}, u32[]{:S(2)}) copy-start(f32[256]{0:T(256)} %param.22) | copy-start | bytes 3076
  9.5 0.7 %copy-start.11 = (f32[256]{0:T(256)S(1)}, f32[256]{0:T(256)}, u32[]{:S(2)}) copy-start(f32[256]{0:T(256)} %param.23) | copy-start | bytes 3076
  10.2 0.7 %copy-start.12 = (f32[256]{0:T(256)S(1)}, f32[256]{0:T(256)}, u32[]{:S(2)}) copy-start(f32[256]{0:T(256)} %param.27) | copy-start | bytes 3076
  10.9 0.7 %copy-start.13 = (f32[256]{0:T(256)S(1)}, f32[256]{0:T(256)}, u32[]{:S(2)}) copy-start(f32[256]{0:T(256)} %param.28) | copy-start | bytes 3076
  11.5 0.7 %copy-start.14 = (f32[256]{0:T(256)S(1)}, f32[256]{0:T(256)}, u32[]{:S(2)}) copy-start(f32[256]{0:T(256)} %param.29) | copy-start | bytes 3076

commit v2 on v1

v2 whole, which is shorter than its diff:
```python
import functools

import jax
import jax.numpy as jnp
from jax import lax
from jax.experimental import pallas as pl
from jax.experimental.pallas import tpu as pltpu
from jax.sharding import PartitionSpec as P

MESH = pl.DeviceIdType.MESH
BF16 = jnp.bfloat16
F32 = jnp.float32

L5, L4, L3, W5, W4A, W3, W4B, PAD, ROWS = 0, 128, 192, 224, 368, 416, 560, 656, 672
WHOLE = {"A": (0, 128), "C": (128, 96)}
QUARTERED = {"P": (224, 48), "Q": (416, 48), "R": (608, 16)}
VMEM_LIMIT = 56 * 1024 * 1024
COPIES = 2 * 31 + 3 * 29
ORDER = [
    "Q0", "P0", "A0", "R0", "C0", "Q1", "P1", "A1", "A2", "A3", "Q2", "R1", "A4", "A5", "P2", "A6", "C1", "C2",
    "A7", "C3", "Q3", "R2", "A8", "M0", "C4", "P3", "C5", "Q4", "C6", "R3", "C7", "P4", "C8", "M1", "H4", "H3",
    "M2", "R4", "Q5", "M3", "Q6", "P5", "R5", "V2", "R6", "P6", "V4", "M4", "V5", "V3",
]


def kernel(
    s3, s4, s5, l3, l4, l5, lb3, lb4, lb5, o3, o4, o5, ob3, ob4, ob5,
    y3, y4, y5, y6,
    x3, x4, x5, held, taps, m3, m4, m5, wide4, wide3, even,
    offsets, own_sem, load_sem, send, recv, m_send, m_recv,
):
    dp, sp = lax.axis_index("dp"), lax.axis_index("space")
    core, x, z_hi = lax.rem(dp, 2), lax.rem(dp // 2, 4), dp // 8
    y, z = sp // 4, lax.rem(sp, 4)

    def along_y(by):
        return dp, lax.rem(y + by + 4, 4) * 4 + z

    def along_x(by):
        return z_hi * 8 + lax.rem(x + by + 4, 4) * 2 + core, sp

    sibling = (dp + 1 - 2 * core, sp)
    below, above = (dp, lax.rem(sp + 1, 16)), (dp, lax.rem(sp + 15, 16))
    in_line = [(dp, y * 4 + lax.rem(z + i, 4)) for i in (1, 2, 3)]

    lanes = pl.ds(pl.multiple_of(core * 128, 128), 128)
    tensors = (
        (l5, 0, L5, L4),
        (l4, 0, L4, L3),
        (l3, 0, L3, W5),
        (o5, 0, W5, W4A),
        (o4, 0, W4A, W3),
        (o3, 0, W3, W4B),
        (o4, 48, W4B, PAD),
        (o4, 0, PAD, ROWS),
    )

    def load_own(number, first, last):
        for ref, skipped, start, end in tensors:
            low, high = max(first, start), min(last, end)
            if low < high:
                pltpu.make_async_copy(
                    ref.at[low - start + skipped : high - start + skipped, lanes],
                    held.at[core, sp, low:high, :],
                    own_sem.at[number],
                ).start()

    stages = list(WHOLE) + list(QUARTERED)
    for name, (first, count) in WHOLE.items():
        load_own(stages.index(name), first, first + count)
    for name, (first, count) in QUARTERED.items():
        for q in range(4):
            at = first + q * count

            @pl.when(x == q)
            def _():
                load_own(stages.index(name), at, at + count)

    section_loads = [
        pltpu.make_async_copy(ref.at[0], to, load_sem.at[i])
        for i, (ref, to) in enumerate(((s5, x5), (s4, x4), (s3, x3)))
    ]
    bias_loads = [
        pltpu.make_async_copy(ref, offsets.at[i : i + 1], load_sem.at[3 + i])
        for i, ref in enumerate((lb3, lb4, lb5, ob3, ob4, ob5))
    ]
    for copy in section_loads + bias_loads:
        copy.start()
    near = [along_y(by) for by in (1, 2, 3)] + [along_x(1), along_x(-1)]
    partners = near + in_line + [sibling]
    barrier = pltpu.get_barrier_semaphore()
    for where in partners:
        pl.semaphore_signal(barrier, inc=1, device_id=where, device_id_type=MESH)

    m5[0] = jnp.zeros_like(m5[0])
    m5[33] = jnp.zeros_like(m5[33])

    for copy in bias_loads:
        copy.wait()
    pl.semaphore_wait(barrier, len(partners))

    sent = []
    numbers = {}

    def copy_of(ref, where, name):
        number = numbers.setdefault(name, len(numbers))
        return pltpu.make_async_remote_copy(
            src_ref=ref,
            dst_ref=ref,
            send_sem=send.at[number],
            recv_sem=recv.at[number],
            device_id=where,
            device_id_type=MESH,
        )

    def go(ref, where, name):
        copy = copy_of(ref, where, name)
        copy.start()
        sent.append(copy)

    def arrived(ref, name):
        copy_of(ref, sibling, name).wait_recv()

    def step(stage, k):
        quartered = stage in QUARTERED
        first, count = QUARTERED[stage] if quartered else WHOLE[stage]

        def rows(by_x=0):
            if not quartered:
                return pl.ds(first, count)
            return pl.ds(pl.multiple_of(first + count * lax.rem(x + by_x, 4), 16), count)

        def slot(by_z, by_y=0, of_core=core):
            at = 4 * lax.rem(y + by_y + 4, 4) + lax.rem(z + by_z + 4, 4)
            return held.at[of_core, at, rows(), :]

        def block(by, by_x=0):
            return held.at[core, pl.ds(4 * lax.rem(y + by, 4), 4), rows(by_x), :]

        def quarter(of_core, by_x):
            return held.at[of_core, :, rows(by_x), :]

        def along_column(i):
            for by in (1, 3) if quartered else (1, 3, 2):
                go(slot(-i), along_y(by), (stage, "y", i, by))

        def half_block(by, at):
            return held.at[core, pl.ds(4 * lax.rem(y + by, 4) + at, 2), rows(), :]

        def pair_along_x(by):
            go(block(by), along_x(1), (stage, "xl", by))
            go(block(by), along_x(-1), (stage, "xr", by))

        if k == 0:
            own = held.at[core, sp, rows(), :]
            pltpu.make_async_copy(own, own, own_sem.at[stages.index(stage)]).wait()
            for i in (1, 2, 3):
                go(own, in_line[i - 1], (stage, "z", i))
            along_column(0)
            if not quartered:
                go(own, sibling, (stage, "c", 0, 0))
        elif not quartered:
            if k <= 3:
                arrived(slot(-k), (stage, "z", k))
                along_column(k)
                go(slot(-k), sibling, (stage, "c", k, 0))
            elif k <= 7:
                for by in (1, 3, 2):
                    arrived(slot(4 - k, -by), (stage, "y", k - 4, by))
                    go(slot(4 - k, -by), sibling, (stage, "c", k - 4, by))
            else:
                for i in range(4):
                    for by in range(4):
                        arrived(slot(-i, -by, 1 - core), (stage, "c", i, by))
        elif k == 1:
            for i in (1, 2, 3):
                arrived(slot(-i), (stage, "z", i))
                along_column(i)
            pair_along_x(0)
        elif k == 2:
            for by, at in ((1, 0), (3, 2)):
                for i in range(4):
                    arrived(slot(-i, -by), (stage, "y", i, by))
                go(half_block(4 - by, at), along_y(by), (stage, "yo", at))
                pair_along_x(4 - by)
        elif k == 3:
            for at in (0, 2):
                arrived(half_block(2, at), (stage, "yo", at))
            pair_along_x(2)
            go(quarter(core, 0), sibling, (stage, "c", 0))
        elif k == 4:
            for by in (0, 3, 1, 2):
                arrived(block(by, 3), (stage, "xl", by))
                if by in (0, 3):
                    go(block(by, 3), along_x(1), (stage, "xo", by))
                arrived(block(by, 1), (stage, "xr", by))
                if by in (1, 2):
                    go(block(by, 1), along_x(-1), (stage, "xo", by))
            go(quarter(core, 3), sibling, (stage, "c", 1))
            go(quarter(core, 1), sibling, (stage, "c", 2))
        elif k == 5:
            for by in (0, 3, 1, 2):
                arrived(block(by, 2), (stage, "xo", by))
            go(quarter(core, 2), sibling, (stage, "c", 3))
        else:
            for i, by_x in enumerate((0, 3, 1, 2)):
                arrived(quarter(1 - core, by_x), (stage, "c", i))

    def weights(first, count, chunks):
        left = jnp.concatenate([held[0, s, first : first + count, :] for s in chunks], axis=0)
        right = jnp.concatenate(
            [held[1, s, first : first + count, :] for s in chunks], axis=0
        )
        return jnp.concatenate([left, right], axis=1)

    def lateral(features, first, count):
        per = 256 // count
        total = None
        for start in range(0, 16, per):
            term = jnp.dot(
                features[:, start * count : (start + per) * count],
                weights(first, count, range(start, start + per)),
                preferred_element_type=F32,
            )
            total = term if total is None else total + term
        return total

    def doubled(field, ref):
        count = field.shape[0]
        for h in range(2):
            for odd in range(2):
                ref[h, pl.ds(odd, count, 2), :] = field[:, 128 * h : 128 * h + 128]

    def doubled_rows(ref, first, count):
        return jnp.concatenate([ref[h, first : first + count, :] for h in range(2)], axis=1)

    m_sent = []

    def m_copy(ref, to, where, index):
        return pltpu.make_async_remote_copy(
            src_ref=ref,
            dst_ref=to,
            send_sem=m_send.at[index],
            recv_sem=m_recv.at[index],
            device_id=where,
            device_id_type=MESH,
        )

    def m_go(ref, to, where, index):
        copy = m_copy(ref, to, where, index)
        copy.start()
        m_sent.append(copy)

    def rows5(first, count):
        return m5.at[pl.ds(1 + first, count)]

    def merge_five():
        section_loads[0].wait()
        merged = lateral(x5[...].reshape(64, 2048), L5, 128) + offsets[2:3]
        rounded = merged.astype(BF16)
        m5[pl.ds(1 + 2 * sp, 2)] = rounded.reshape(2, 32, 256)
        doubled(rounded.astype(F32), wide4)
        own = rows5(2 * sp, 2)
        for i in (1, 2, 3):
            m_go(own, own, in_line[i - 1], i - 1)
        for by in (1, 3, 2):
            m_go(own, own, along_y(by), 2 + by)

    def pass_five(i):
        ref = rows5(8 * y + 2 * lax.rem(z + 4 - i, 4), 2)
        m_copy(ref, ref, sibling, i - 1).wait_recv()
        for by in (1, 3, 2):
            m_go(ref, ref, along_y(by), 2 + 3 * i + by)

    def all_five():
        for i in range(4):
            for by in (1, 3, 2):
                ref = rows5(8 * lax.rem(y + 4 - by, 4) + 2 * lax.rem(z + 4 - i, 4), 2)
                m_copy(ref, ref, sibling, 2 + 3 * i + by).wait_recv()

    def merge_four():
        section_loads[1].wait()
        up = jnp.concatenate([doubled_rows(wide4, 64 * (r // 2), 64) for r in range(4)], axis=0)
        merged = lateral(x4[...].reshape(256, 1024), L4, 64) + offsets[1:2] + up
        rounded = merged.astype(BF16)
        m4[1:5] = rounded.reshape(4, 64, 256)
        m_go(m4.at[4:5], m4.at[0:1], below, 15)
        m_go(m4.at[1:2], m4.at[5:6], above, 16)
        doubled(rounded.astype(F32), wide3)

    def merge_three():
        section_loads[2].wait()
        for r in (0, 3, 1, 2):
            up = doubled_rows(wide3, 128 * r, 128)
            merged = lateral(x3[2 * r : 2 * r + 2].reshape(256, 512), L3, 32) + offsets[0:1]
            merged = merged + jnp.concatenate([up, up], axis=0)
            m3[1 + 2 * r : 3 + 2 * r] = merged.astype(BF16).reshape(2, 128, 256)
        m_go(m3.at[8:9], m3.at[0:1], below, 17)
        m_go(m3.at[1:2], m3.at[9:10], above, 18)

    def rims(ref, index, last):
        m_copy(ref.at[0:1], ref.at[0:1], below, index).wait_recv()
        m_copy(ref.at[last : last + 1], ref.at[last : last + 1], below, index + 1).wait_recv()

        @pl.when(sp == 0)
        def _():
            ref[0] = jnp.zeros_like(ref[0])

        @pl.when(sp == 15)
        def _():
            ref[last] = jnp.zeros_like(ref[last])

    def prepare(level, tap_rows):
        for c in range(3):
            for r in range(3):
                taps[level, c, 256 * r : 256 * r + 256, :] = weights(tap_rows[3 * r + c], 16, range(16))

    def conv(level, ref, starts, columns, offset, each, keep):
        count = each * columns
        column = lax.rem(lax.broadcasted_iota(jnp.int32, (count, 256), 0), columns)
        for start in starts:
            window = jnp.concatenate(
                [ref[start + r : start + r + each].reshape(count, 256) for r in range(3)], axis=1
            )
            parts = [jnp.dot(window, taps[level, c], preferred_element_type=F32) for c in range(3)]
            left = jnp.where(column == 0, 0.0, pltpu.roll(parts[0], 1, 0))
            right = jnp.where(column == columns - 1, 0.0, pltpu.roll(parts[2], count - 1, 0))
            summed = parts[1] + offsets[offset : offset + 1] + left + right
            keep(start, summed.astype(BF16).reshape(each, columns, 256))

    def keep5(start, rounded):
        y5[start : start + 8] = rounded
        for r in range(0, 8, 2):
            for h in range(2):
                even[h, 16 * r : 16 * r + 32, :] = rounded[r, :, 128 * h : 128 * h + 128].astype(F32)
        for h in range(2):
            picked = even[h, pl.ds(0, 64, 2), :].astype(BF16).reshape(4, 16, 128)
            y6[start // 2 : start // 2 + 4, :, 128 * h : 128 * h + 128] = picked

    def keep3(start, rounded):
        y3[start : start + 2] = rounded

    def keep4(start, rounded):
        y4[start : start + 4] = rounded

    def five():
        prepare(2, range(W5, W4A, 16))
        conv(2, m5, range(0, 32, 8), 32, 5, 8, keep5)

    def inner_three():
        prepare(0, range(W3, W4B, 16))
        conv(0, m3, (2, 4), 128, 3, 2, keep3)

    def outer_three():
        rims(m3, 17, 9)
        conv(0, m3, (0, 6), 128, 3, 2, keep3)

    def four():
        prepare(1, [*range(W4A, W3, 16), *range(W4B, PAD, 16)])
        rims(m4, 15, 5)
        conv(1, m4, (0,), 64, 4, 4, keep4)

    others = {
        "M0": merge_five,
        "M1": functools.partial(pass_five, 1),
        "M2": functools.partial(pass_five, 2),
        "M3": functools.partial(pass_five, 3),
        "M4": all_five,
        "H4": merge_four,
        "H3": merge_three,
        "V5": five,
        "V2": inner_three,
        "V3": outer_three,
        "V4": four,
    }
    for name in ORDER:
        if name in others:
            others[name]()
        else:
            step(name[0], int(name[1]))
    for copy in sent + m_sent:
        copy.wait_send()


def mover(a, b, c, d, to_a, to_b, to_c, to_d, sem):
    copies = [
        pltpu.make_async_copy(ref, to.at[0], sem.at[i])
        for i, (ref, to) in enumerate(((a, to_a), (b, to_b), (c, to_c), (d, to_d)))
    ]
    for copy in copies:
        copy.start()
    for copy in copies:
        copy.wait()


def on_device(
    section_three,
    section_four,
    section_five,
    lateral_three,
    lateral_four,
    lateral_five,
    lateral_bias_three,
    lateral_bias_four,
    lateral_bias_five,
    output_three,
    output_four,
    output_five,
    output_bias_three,
    output_bias_four,
    output_bias_five,
):
    anywhere = pl.BlockSpec(memory_space=pl.ANY)
    row = [bias.reshape(1, 256) for bias in (
        lateral_bias_three, lateral_bias_four, lateral_bias_five,
        output_bias_three, output_bias_four, output_bias_five)]
    dma = pltpu.SemaphoreType.DMA
    held_results = pl.pallas_call(
        kernel,
        out_shape=(
            pltpu.VMEM((8, 128, 256), BF16),
            pltpu.VMEM((4, 64, 256), BF16),
            pltpu.VMEM((32, 32, 256), BF16),
            pltpu.VMEM((16, 16, 256), BF16),
        ),
        in_specs=[anywhere] * 15,
        out_specs=(pl.BlockSpec(memory_space=pltpu.VMEM),) * 4,
        scratch_shapes=[
            pltpu.VMEM((8, 128, 512), BF16),
            pltpu.VMEM((4, 64, 1024), BF16),
            pltpu.VMEM((2, 32, 2048), BF16),
            pltpu.VMEM((2, 16, ROWS, 128), BF16),
            pltpu.VMEM((3, 3, 768, 256), BF16),
            pltpu.VMEM((10, 128, 256), BF16),
            pltpu.VMEM((6, 64, 256), BF16),
            pltpu.VMEM((34, 32, 256), BF16),
            pltpu.VMEM((2, 128, 128), F32),
            pltpu.VMEM((2, 512, 128), F32),
            pltpu.VMEM((2, 128, 128), F32),
            pltpu.VMEM((6, 256), F32),
            dma((5,)),
            dma((9,)),
            dma((COPIES,)),
            dma((COPIES,)),
            dma((19,)),
            dma((19,)),
        ],
        compiler_params=pltpu.CompilerParams(
            collective_id=0, has_side_effects=True, vmem_limit_bytes=VMEM_LIMIT
        ),
    )(
        section_three, section_four, section_five,
        lateral_three, lateral_four, lateral_five, row[0], row[1], row[2],
        output_three.reshape(144, 256), output_four.reshape(144, 256),
        output_five.reshape(144, 256), row[3], row[4], row[5],
    )
    return pl.pallas_call(
        mover,
        out_shape=tuple(jax.ShapeDtypeStruct((1, *one.shape), BF16) for one in held_results),
        in_specs=[anywhere] * 4,
        out_specs=(anywhere,) * 4,
        scratch_shapes=[dma((4,))],
        compiler_params=pltpu.CompilerParams(vmem_limit_bytes=1024 * 1024),
    )(*held_results)


def solution(mesh):
    return jax.shard_map(
        on_device,
        mesh=mesh,
        in_specs=(
            P("dp", "space", None, None),
            P("dp", "space", None, None),
            P("dp", "space", None, None),
            P("space", None),
            P("space", None),
            P("space", None),
            P(),
            P(),
            P(),
            P(None, None, "space", None),
            P(None, None, "space", None),
            P(None, None, "space", None),
            P(),
            P(),
            P(),
        ),
        out_specs=(
            P("dp", "space", None, None),
            P("dp", "space", None, None),
            P("dp", None, None, None),
            P("dp", None, None, None),
        ),
        check_vma=False,
    )
```

time: 67.4 us -> 43.6 us (0.65)
  local copies, waits for them, and re-layouts: 14.5 us -> 0 us
  Pallas kernels: 51.7 us -> 42.9 us
    unnamed x34 -> x0, local copies, waits for them, and re-layouts: 14.5 us -> none
    pallas_call x1 -> x2, Pallas kernels: 51.7 us -> 42.9 us  [the longest x1 41.8 us: on_device(): pl.pallas_call(kernel, out_shape=(pltpu.VMEM((8, 128, 256), BF16), pltpu....]
where the time goes in v2:
time: 43.6 us; the launch traced here: 43.5 us
  Pallas kernels  42.9 us (98%)
  between operations  0.65 us (1%)
    pallas_call x1, Pallas kernels, on_device(): pl.pallas_call(kernel, out_shape=(pltpu.VMEM((8, 128, 256), BF16), pltpu....  41.8 us
    pallas_call x1, Pallas kernels, on_device(): pl.pallas_call(mover, out_shape=tuple((jax.ShapeDtypeStruct((1, *one.shap...  1.08 us

profile of v2, /device:TPU:1, one launch (start us, length us, event | category | flops | bytes accessed | tf_op | source)
XLA Modules:
  0.0 43.5 jit_solution(8714892573387491850)
XLA Ops:
  0.6 41.8 %shard_map.174 = (bf16[8,128,256]{2,1,0:T(8,128)(2,1)S(1)}, bf16[4,64,256]{2,1,0:T(8,128)(2,1)S(1)}, bf16[32,32,256]{2,1,0:T(8,128)(2,1)S(1)}, bf16[16,16,256]{2,1,0:T(8,128)(2,1)S(1)}) custom-call(bf16[1,8,128,512]{3,2,1,0:T(8,128)(2,1)} %s3.1, bf16[1,4,64,1024]{3,2,1,0:T(8,128)(2,1)} %s4_.1, bf16[1,2,32,2048]{3,2,1,0:T(8,128)(2,1)} %s5.1, ...), custom_call_target="tpu_custom_call" | custom-call | tf_op jit(solution)/shard_map/pallas_call | solution.py:418
  42.5 1.1 %shard_map.175 = (bf16[1,8,128,256]{3,2,1,0:T(8,128)(2,1)}, bf16[1,4,64,256]{3,2,1,0:T(8,128)(2,1)}, bf16[1,32,32,256]{3,2,1,0:T(8,128)(2,1)}, bf16[1,16,16,256]{3,2,1,0:T(8,128)(2,1)}) custom-call(bf16[8,128,256]{2,1,0:T(8,128)(2,1)S(1)} %get-tuple-element.8.a, bf16[4,64,256]{2,1,0:T(8,128)(2,1)S(1)} %get-tuple-element.9.b, ...), custom_call_target="tpu_custom_call" | custom-call | tf_op jit(solution)/shard_map/pallas_call | solution.py:457

commit v3 on v2

--- a/solution.py
+++ b/solution.py
@@ -13,13 +13,15 @@
 
 L5, L4, L3, W5, W4A, W3, W4B, PAD, ROWS = 0, 128, 192, 224, 368, 416, 560, 656, 672
 WHOLE = {"A": (0, 128), "C": (128, 96)}
-QUARTERED = {"P": (224, 48), "Q": (416, 48), "R": (608, 16)}
+PARTED = {"P": (224, 48, 4), "Q": (416, 48, 4), "R": (608, 32, 2)}
+ONE_HOP = ["P", "R"]
 VMEM_LIMIT = 56 * 1024 * 1024
-COPIES = 2 * 31 + 3 * 29
+COPIES = 160
+SETTLED = 16
 ORDER = [
-    "Q0", "P0", "A0", "R0", "C0", "Q1", "P1", "A1", "A2", "A3", "Q2", "R1", "A4", "A5", "P2", "A6", "C1", "C2",
-    "A7", "C3", "Q3", "R2", "A8", "M0", "C4", "P3", "C5", "Q4", "C6", "R3", "C7", "P4", "C8", "M1", "H4", "H3",
-    "M2", "R4", "Q5", "M3", "Q6", "P5", "R5", "V2", "R6", "P6", "V4", "M4", "V5", "V3",
+    "Q0", "P0", "A0", "C0", "R0", "Q1", "P1", "A1", "A2", "A3", "P2", "A4", "Q2", "C1", "P3", "A5", "A6", "C2",
+    "C3", "A7", "R1", "Q3", "A8", "M0", "P4", "C4", "C5", "C6", "C7", "Q4", "R2", "C8", "H4", "M1", "R3", "M2",
+    "H3", "M3", "Q5", "R4", "Q6", "T3", "P5", "V2", "R5", "P6", "T4", "T5", "V4", "S0", "M4", "V5", "V3",
 ]
 
 
@@ -42,6 +44,12 @@
     sibling = (dp + 1 - 2 * core, sp)
     below, above = (dp, lax.rem(sp + 1, 16)), (dp, lax.rem(sp + 15, 16))
     in_line = [(dp, y * 4 + lax.rem(z + i, 4)) for i in (1, 2, 3)]
+
+    near = [along_y(by) for by in (1, 2, 3)] + [along_x(1), along_x(-1)]
+    partners = near + in_line + [sibling]
+    barrier = pltpu.get_barrier_semaphore()
+    for where in partners:
+        pl.semaphore_signal(barrier, inc=1, device_id=where, device_id_type=MESH)
 
     lanes = pl.ds(pl.multiple_of(core * 128, 128), 128)
     tensors = (
@@ -65,14 +73,14 @@
                     own_sem.at[number],
                 ).start()
 
-    stages = list(WHOLE) + list(QUARTERED)
+    stages = list(WHOLE) + list(PARTED)
     for name, (first, count) in WHOLE.items():
         load_own(stages.index(name), first, first + count)
-    for name, (first, count) in QUARTERED.items():
-        for q in range(4):
+    for name, (first, count, parts) in PARTED.items():
+        for q in range(parts):
             at = first + q * count
 
-            @pl.when(x == q)
+            @pl.when(lax.rem(x, parts) == q)
             def _():
                 load_own(stages.index(name), at, at + count)
 
@@ -86,17 +94,9 @@
     ]
     for copy in section_loads + bias_loads:
         copy.start()
-    near = [along_y(by) for by in (1, 2, 3)] + [along_x(1), along_x(-1)]
-    partners = near + in_line + [sibling]
-    barrier = pltpu.get_barrier_semaphore()
-    for where in partners:
-        pl.semaphore_signal(barrier, inc=1, device_id=where, device_id_type=MESH)
-
     m5[0] = jnp.zeros_like(m5[0])
     m5[33] = jnp.zeros_like(m5[33])
 
-    for copy in bias_loads:
-        copy.wait()
     pl.semaphore_wait(barrier, len(partners))
 
     sent = []
@@ -122,13 +122,13 @@
         copy_of(ref, sibling, name).wait_recv()
 
     def step(stage, k):
-        quartered = stage in QUARTERED
-        first, count = QUARTERED[stage] if quartered else WHOLE[stage]
+        first, count, parts = PARTED[stage] if stage in PARTED else (*WHOLE[stage], 1)
+        one_hop = parts == 1 or stage in ONE_HOP
 
         def rows(by_x=0):
-            if not quartered:
+            if parts == 1:
                 return pl.ds(first, count)
-            return pl.ds(pl.multiple_of(first + count * lax.rem(x + by_x, 4), 16), count)
+            return pl.ds(pl.multiple_of(first + count * lax.rem(x + by_x, parts), 16), count)
 
         def slot(by_z, by_y=0, of_core=core):
             at = 4 * lax.rem(y + by_y + 4, 4) + lax.rem(z + by_z + 4, 4)
@@ -137,19 +137,21 @@
         def block(by, by_x=0):
             return held.at[core, pl.ds(4 * lax.rem(y + by, 4), 4), rows(by_x), :]
 
-        def quarter(of_core, by_x):
+        def part(of_core, by_x):
             return held.at[of_core, :, rows(by_x), :]
 
         def along_column(i):
-            for by in (1, 3) if quartered else (1, 3, 2):
+            for by in (1, 3, 2) if one_hop else (1, 3):
                 go(slot(-i), along_y(by), (stage, "y", i, by))
 
         def half_block(by, at):
             return held.at[core, pl.ds(4 * lax.rem(y + by, 4) + at, 2), rows(), :]
 
         def pair_along_x(by):
-            go(block(by), along_x(1), (stage, "xl", by))
-            go(block(by), along_x(-1), (stage, "xr", by))
+            if parts == 4 or by in (0, 3):
+                go(block(by), along_x(1), (stage, "xl", by))
+            if parts == 4 or by in (1, 2):
+                go(block(by), along_x(-1), (stage, "xr", by))
 
         if k == 0:
             own = held.at[core, sp, rows(), :]
@@ -157,9 +159,9 @@
             for i in (1, 2, 3):
                 go(own, in_line[i - 1], (stage, "z", i))
             along_column(0)
-            if not quartered:
+            if parts == 1:
                 go(own, sibling, (stage, "c", 0, 0))
-        elif not quartered:
+        elif parts == 1:
             if k <= 3:
                 arrived(slot(-k), (stage, "z", k))
                 along_column(k)
@@ -181,13 +183,25 @@
             for by, at in ((1, 0), (3, 2)):
                 for i in range(4):
                     arrived(slot(-i, -by), (stage, "y", i, by))
-                go(half_block(4 - by, at), along_y(by), (stage, "yo", at))
+                if not one_hop:
+                    go(half_block(4 - by, at), along_y(by), (stage, "yo", at))
                 pair_along_x(4 - by)
         elif k == 3:
-            for at in (0, 2):
-                arrived(half_block(2, at), (stage, "yo", at))
+            if one_hop:
+                for i in range(4):
+                    arrived(slot(-i, -2), (stage, "y", i, 2))
+            else:
+                for at in (0, 2):
+                    arrived(half_block(2, at), (stage, "yo", at))
             pair_along_x(2)
-            go(quarter(core, 0), sibling, (stage, "c", 0))
+            go(part(core, 0), sibling, (stage, "c", 0))
+        elif k == 4 and parts == 2:
+            for by in (0, 3, 1, 2):
+                arrived(block(by, 1), (stage, "xl" if by in (0, 3) else "xr", by))
+            go(part(core, 1), sibling, (stage, "c", 1))
+        elif k == 5 and parts == 2:
+            for by_x in range(2):
+                arrived(part(1 - core, by_x), (stage, "c", by_x))
         elif k == 4:
             for by in (0, 3, 1, 2):
                 arrived(block(by, 3), (stage, "xl", by))
@@ -196,15 +210,15 @@
                 arrived(block(by, 1), (stage, "xr", by))
                 if by in (1, 2):
                     go(block(by, 1), along_x(-1), (stage, "xo", by))
-            go(quarter(core, 3), sibling, (stage, "c", 1))
-            go(quarter(core, 1), sibling, (stage, "c", 2))
+            go(part(core, 3), sibling, (stage, "c", 1))
+            go(part(core, 1), sibling, (stage, "c", 2))
         elif k == 5:
             for by in (0, 3, 1, 2):
                 arrived(block(by, 2), (stage, "xo", by))
-            go(quarter(core, 2), sibling, (stage, "c", 3))
+            go(part(core, 2), sibling, (stage, "c", 3))
         else:
             for i, by_x in enumerate((0, 3, 1, 2)):
-                arrived(quarter(1 - core, by_x), (stage, "c", i))
+                arrived(part(1 - core, by_x), (stage, "c", i))
 
     def weights(first, count, chunks):
         left = jnp.concatenate([held[0, s, first : first + count, :] for s in chunks], axis=0)
@@ -256,6 +270,8 @@
 
     def merge_five():
         section_loads[0].wait()
+        for copy in bias_loads:
+            copy.wait()
         merged = lateral(x5[...].reshape(64, 2048), L5, 128) + offsets[2:3]
         rounded = merged.astype(BF16)
         m5[pl.ds(1 + 2 * sp, 2)] = rounded.reshape(2, 32, 256)
@@ -344,11 +360,9 @@
         y4[start : start + 4] = rounded
 
     def five():
-        prepare(2, range(W5, W4A, 16))
         conv(2, m5, range(0, 32, 8), 32, 5, 8, keep5)
 
     def inner_three():
-        prepare(0, range(W3, W4B, 16))
         conv(0, m3, (2, 4), 128, 3, 2, keep3)
 
     def outer_three():
@@ -356,11 +370,19 @@
         conv(0, m3, (0, 6), 128, 3, 2, keep3)
 
     def four():
-        prepare(1, [*range(W4A, W3, 16), *range(W4B, PAD, 16)])
         rims(m4, 15, 5)
         conv(1, m4, (0,), 64, 4, 4, keep4)
 
+    def settle():
+        for copy in sent[:-SETTLED]:
+            copy.wait_send()
+        del sent[:-SETTLED]
+
     others = {
+        "T5": functools.partial(prepare, 2, range(W5, W4A, 16)),
+        "T3": functools.partial(prepare, 0, range(W3, W4B, 16)),
+        "T4": functools.partial(prepare, 1, [*range(W4A, W3, 16), *range(W4B, PAD, 16)]),
+        "S0": settle,
         "M0": merge_five,
         "M1": functools.partial(pass_five, 1),
         "M2": functools.partial(pass_five, 2),

time: 43.6 us -> 41.9 us (0.961)
  Pallas kernels: 42.9 us -> 41.1 us
    pallas_call x1, Pallas kernels: 41.8 us -> 40.1 us  [on_device(): pl.pallas_call(kernel, out_shape=(pltpu.VMEM((8, 128, 256), BF16), pltpu....]
where the time goes in v3:
time: 41.9 us; the launch traced here: 41.8 us
  Pallas kernels  41.1 us (98%)
  between operations  0.65 us (2%)
    pallas_call x1, Pallas kernels, on_device(): pl.pallas_call(kernel, out_shape=(pltpu.VMEM((8, 128, 256), BF16), pltpu....  40.1 us
    pallas_call x1, Pallas kernels, on_device(): pl.pallas_call(mover, out_shape=tuple((jax.ShapeDtypeStruct((1, *one.shap...  1.08 us

profile of v3, /device:TPU:1, one launch (start us, length us, event | category | flops | bytes accessed | tf_op | source)
XLA Modules:
  0.0 41.8 jit_solution(15333668207287136834)
XLA Ops:
  0.6 40.1 %shard_map.174 = (bf16[8,128,256]{2,1,0:T(8,128)(2,1)S(1)}, bf16[4,64,256]{2,1,0:T(8,128)(2,1)S(1)}, bf16[32,32,256]{2,1,0:T(8,128)(2,1)S(1)}, bf16[16,16,256]{2,1,0:T(8,128)(2,1)S(1)}) custom-call(bf16[1,8,128,512]{3,2,1,0:T(8,128)(2,1)} %s3.1, bf16[1,4,64,1024]{3,2,1,0:T(8,128)(2,1)} %s4_.1, bf16[1,2,32,2048]{3,2,1,0:T(8,128)(2,1)} %s5.1, ...), custom_call_target="tpu_custom_call" | custom-call | tf_op jit(solution)/shard_map/pallas_call | solution.py:440
  40.7 1.1 %shard_map.175 = (bf16[1,8,128,256]{3,2,1,0:T(8,128)(2,1)}, bf16[1,4,64,256]{3,2,1,0:T(8,128)(2,1)}, bf16[1,32,32,256]{3,2,1,0:T(8,128)(2,1)}, bf16[1,16,16,256]{3,2,1,0:T(8,128)(2,1)}) custom-call(bf16[8,128,256]{2,1,0:T(8,128)(2,1)S(1)} %get-tuple-element.8.a, bf16[4,64,256]{2,1,0:T(8,128)(2,1)S(1)} %get-tuple-element.9.b, ...), custom_call_target="tpu_custom_call" | custom-call | tf_op jit(solution)/shard_map/pallas_call | solution.py:479

commit v4 on v3

--- a/solution.py
+++ b/solution.py
@@ -20,7 +20,7 @@
 SETTLED = 16
 ORDER = [
     "Q0", "P0", "A0", "C0", "R0", "Q1", "P1", "A1", "A2", "A3", "P2", "A4", "Q2", "C1", "P3", "A5", "A6", "C2",
-    "C3", "A7", "R1", "Q3", "A8", "M0", "P4", "C4", "C5", "C6", "C7", "Q4", "R2", "C8", "H4", "M1", "R3", "M2",
+    "C3", "A7", "R1", "Q3", "A8", "M0", "P4", "C4", "C5", "C6", "C7", "Q4", "R2", "M1", "C8", "H4", "R3", "M2",
     "H3", "M3", "Q5", "R4", "Q6", "T3", "P5", "V2", "R5", "P6", "T4", "T5", "V4", "S0", "M4", "V5", "V3",
 ]
 

time: 41.9 us -> 41.7 us (level)
  no operation moved by 1% of the time
where the time goes in v4:
time: 41.7 us; the launch traced here: 41.6 us
  Pallas kernels  41 us (98%)
  between operations  0.65 us (2%)
    pallas_call x1, Pallas kernels, on_device(): pl.pallas_call(kernel, out_shape=(pltpu.VMEM((8, 128, 256), BF16), pltpu....  39.9 us
    pallas_call x1, Pallas kernels, on_device(): pl.pallas_call(mover, out_shape=tuple((jax.ShapeDtypeStruct((1, *one.shap...  1.08 us

profile of v4, /device:TPU:1, one launch (start us, length us, event | category | flops | bytes accessed | tf_op | source)
XLA Modules:
  0.0 41.6 jit_solution(10279558215633208859)
XLA Ops:
  0.6 39.9 %shard_map.174 = (bf16[8,128,256]{2,1,0:T(8,128)(2,1)S(1)}, bf16[4,64,256]{2,1,0:T(8,128)(2,1)S(1)}, bf16[32,32,256]{2,1,0:T(8,128)(2,1)S(1)}, bf16[16,16,256]{2,1,0:T(8,128)(2,1)S(1)}) custom-call(bf16[1,8,128,512]{3,2,1,0:T(8,128)(2,1)} %s3.1, bf16[1,4,64,1024]{3,2,1,0:T(8,128)(2,1)} %s4_.1, bf16[1,2,32,2048]{3,2,1,0:T(8,128)(2,1)} %s5.1, ...), custom_call_target="tpu_custom_call" | custom-call | tf_op jit(solution)/shard_map/pallas_call | solution.py:440
  40.5 1.1 %shard_map.175 = (bf16[1,8,128,256]{3,2,1,0:T(8,128)(2,1)}, bf16[1,4,64,256]{3,2,1,0:T(8,128)(2,1)}, bf16[1,32,32,256]{3,2,1,0:T(8,128)(2,1)}, bf16[1,16,16,256]{3,2,1,0:T(8,128)(2,1)}) custom-call(bf16[8,128,256]{2,1,0:T(8,128)(2,1)S(1)} %get-tuple-element.8.a, bf16[4,64,256]{2,1,0:T(8,128)(2,1)S(1)} %get-tuple-element.9.b, ...), custom_call_target="tpu_custom_call" | custom-call | tf_op jit(solution)/shard_map/pallas_call | solution.py:479
